TPU v7x, 128 devices: a whole 4x4x4 slice. The times are simulated.
128 devices in a mesh: row: 8 (over z_hi, y), col: 16 (over x, z_lo, core).
Axes of the slice: x: 4, y: 4, z: 4 (z_hi: 2, z_lo: 2; z = z_hi * 2 + z_lo), core: 2. Of those that a mesh axis runs over, the one named last changes fastest.
Arguments:
- noise: float32 [4096, 3072], P('row', 'col'), may hold values from -30 to 30
- images: float32 [12288, 3072], P('col', 'row'), may hold values from -6 to 6
- time_index: int32 [4096], P('row'), may hold values from 0 to 999
- w_in: float32 [3072, 3072], P(None, 'col'), may hold values from -0.109375 to 0.109375
- time_gain: float32 [3072], P('col'), may hold values from -5 to 5
- w_out: float32 [3072, 3072], P('col'), may hold values from -0.109375 to 0.109375
Outputs:
- targets: float32 [4096, 3072], P('row', 'col')
- row_pot: float32 [4096], P('row')
- col_pot: float32 [12288], P('col')
- grad_in: float32 [3072, 3072], P('row', 'col')
- grad_time: float32 [3072], P('col')
- grad_out: float32 [3072, 3072], P('col', 'row')
- mse: float32 [], replicated
All inputs are finite; a program needn't handle non-finite values.
Results may differ from a plain program's by a relative error of at most 0.0003.
Values sent between devices are 32-bit elements; how exact they have to be, the bound alone decides.
No kernel may reach another device: no remote copies, remote signals or barrier semaphores. Data moves between devices by JAX's collectives and lax.ppermute only.
A program may use at most 128 MiB of HBM per device.

v0:
```python
import jax
import jax.numpy as jnp
from jax import lax
from jax.sharding import Mesh
from jax.sharding import PartitionSpec as P

ITERS = 2
TIMES = 1000
COL = ("col_0", "col_1", "col_2")


EPSILON = 0.01


def sent_to_all(array, axis):
    devices = lax.axis_size(axis)
    return lax.all_to_all(
        jnp.broadcast_to(array[None], (devices, *array.shape)), axis, 0, 0, tiled=True
    )


def all_in_one(array, axis):
    leaves = jax.tree.leaves(array)
    turns = sorted(range(len(leaves)), key=lambda k: -leaves[k].size)
    width = (1, *leaves[turns[0]].shape)[-1]
    lines = [
        jnp.pad(leaves[k].reshape(-1), (0, -leaves[k].size % width)).reshape(-1, width)
        for k in turns
    ]
    both, at, found = (sent_to_all(jnp.concatenate(lines), axis), 0, {})
    for k, line in zip(turns, lines):
        section = both[:, at : at + len(line)].reshape(len(both), -1)
        found[k] = section[:, : leaves[k].size].reshape(-1, *leaves[k].shape)
        at += len(line)
    numbers = iter(range(len(leaves)))
    return jax.tree.map(lambda _: found[next(numbers)], array)


def once_a_type(array, axis):
    leaves, found = (jax.tree.leaves(array), {})
    for first, a in enumerate(leaves):
        if first not in found:
            alike = [k for k, b in enumerate(leaves) if b.dtype == a.dtype]
            got = (
                all_in_one([leaves[k] for k in alike], axis)
                if len(alike) > 1
                else [sent_to_all(a, axis)]
            )
            for k, b in zip(alike, got):
                found[k] = b
    numbers = iter(range(len(leaves)))
    return jax.tree.map(lambda _: found[next(numbers)], array)


def combined_pairwise(pieces, combine):
    while len(jax.tree.leaves(pieces)[0]) > 1:
        pieces = jax.vmap(combine)(
            *(jax.tree.map(lambda part: part[side::2], pieces) for side in (0, 1))
        )
    return jax.tree.map(lambda part: part[0], pieces)


def joined_all(array, axis, combine):
    pieces = once_a_type(array, axis)
    return combined_pairwise(pieces, combine)


def in_blocks(array, dim, devices):
    shape = array.shape
    tiles = array.reshape(*shape[:dim], devices, shape[dim] // devices, *shape[dim + 1 :])
    return jnp.moveaxis(tiles, dim, 0)


def scatter_pairs(array, chips, core, dim):
    sizes = (lax.axis_size(chips), lax.axis_size(core))
    tiles = in_blocks(array, dim, sizes[0] * sizes[1])
    inside = tiles.shape[1:]
    tiles = tiles.reshape(*sizes, *inside).swapaxes(0, 1).reshape(-1, *inside)
    tiles = lax.psum_scatter(tiles, core, scatter_dimension=0, tiled=True)
    return lax.psum_scatter(tiles, chips, scatter_dimension=0, tiled=True)[0]


def of_everyone(array, axis):
    everything = sent_to_all(array, axis)
    return jnp.sum(everything, axis=0)


def one_scatter(arrays, axis, dims):
    devices = lax.axis_size(axis)
    tiles = [in_blocks(a, dim, devices) for a, dim in zip(arrays, dims)]
    lines = jnp.concatenate([b.reshape(devices, -1) for b in tiles], axis=1)
    rows = max(16, -(-lines.shape[1] // 1024) * 8)
    lines = jnp.pad(lines, ((0, 0), (0, rows * 128 - lines.shape[1]))).reshape(-1, 128)
    flat, at, gathered = (lax.psum_scatter(lines, axis, tiled=True).reshape(-1), 0, [])
    for b in tiles:
        part = b[0]
        gathered.append(flat[at : at + part.size].reshape(part.shape))
        at += part.size
    return tuple(gathered)


def packed_total(arrays, axis):
    flat, at, gathered = (jnp.concatenate([a.reshape(-1) for a in arrays]), 0, [])
    subtotal = of_everyone(flat, axis)
    for a in arrays:
        gathered.append(subtotal[at : at + a.size].reshape(a.shape))
        at += a.size
    return tuple(gathered)


def joined(left_pair, right_pair):
    peak = jnp.maximum(left_pair[0], right_pair[0])
    total = left_pair[1] * jnp.exp(left_pair[0] - peak) + right_pair[1] * jnp.exp(
        right_pair[0] - peak
    )
    return (peak, total)


def over_images(logits):
    local_peak = jnp.max(logits, axis=1)
    local_total = jnp.sum(jnp.exp(logits - local_peak[:, None]), axis=1)
    peak, total = joined_all((local_peak, local_total), COL, joined)
    return (peak, total)


def over_noise(logits):
    local_peak = jnp.max(logits, axis=0)
    local_total = jnp.sum(jnp.exp(logits - local_peak[None, :]), axis=0)
    peak, total = joined_all((local_peak, local_total), "row", joined)
    return (peak, total)


def body(noise, images, time_index, w_in, time_gain, w_out):
    highest = lax.Precision.HIGHEST
    full_noise = lax.all_gather(noise, COL, axis=1, tiled=True)
    full_images = lax.all_gather(images, "row", axis=1, tiled=True)
    width = full_noise.shape[1]
    noise_count = full_noise.shape[0] * lax.axis_size("row")
    image_count = full_images.shape[0] * lax.axis_size(COL)
    noise_norms = jnp.sum(full_noise * full_noise, axis=1)
    image_norms = jnp.sum(full_images * full_images, axis=1)
    cross = lax.dot_general(
        full_noise,
        full_images,
        (((1,), (1,)), ((), ())),
        precision=highest,
        preferred_element_type=jnp.float32,
    )
    scaled = (noise_norms[:, None] + image_norms[None, :] - 2.0 * cross) / (width * EPSILON)
    col_pot = jnp.zeros((full_images.shape[0],), jnp.float32)
    row_pot = jnp.zeros((full_noise.shape[0],), jnp.float32)
    for iteration in range(ITERS):
        peak, total = over_images(col_pot[None, :] - scaled)
        row_pot = jnp.log(jnp.float32(image_count)) - (jnp.log(total) + peak)
        peak, total = over_noise(row_pot[:, None] - scaled)
        col_pot = jnp.log(jnp.float32(noise_count)) - (jnp.log(total) + peak)
    logits = col_pot[None, :] - scaled
    peak, total = over_images(logits)
    weights = jnp.exp(logits - (jnp.log(total) + peak)[:, None])
    partial_value = jnp.dot(
        weights, full_images, precision=highest, preferred_element_type=jnp.float32
    )
    slice_width = noise.shape[1]
    slice_start = lax.axis_index(COL) * slice_width
    targets = lax.psum_scatter(partial_value, COL, scatter_dimension=1, tiled=True)
    whole_targets = lax.all_gather(targets, COL, axis=1, tiled=True)
    fraction = (time_index.astype(jnp.float32) + 0.5) / TIMES
    mixed = (1.0 - fraction)[:, None] * full_noise + fraction[:, None] * whole_targets
    velocity = whole_targets - full_noise
    pre = (
        jnp.dot(mixed, w_in, precision=highest, preferred_element_type=jnp.float32)
        + fraction[:, None] * time_gain[None, :]
    )
    sigma = jax.nn.sigmoid(pre)
    hidden = pre * sigma
    part_out = jnp.dot(hidden, w_out, precision=highest, preferred_element_type=jnp.float32)
    out_share = scatter_pairs(part_out, ("col_0", "col_1"), "col_2", 1)
    diff_share = out_share - lax.dynamic_slice_in_dim(velocity, slice_start, slice_width, 1)
    squared = of_everyone(jnp.sum(diff_share * diff_share), COL)
    slope = lax.all_gather(diff_share / jnp.sqrt(jnp.float32(noise_count)), COL, axis=1, tiled=True)
    local_out = lax.dot_general(
        hidden,
        slope,
        (((0,), (0,)), ((), ())),
        precision=highest,
        preferred_element_type=jnp.float32,
    )
    back = lax.dot_general(
        slope,
        w_out,
        (((1,), (1,)), ((), ())),
        precision=highest,
        preferred_element_type=jnp.float32,
    )
    dpre = back * sigma * (1.0 + pre * (1.0 - sigma))
    local_in = lax.dot_general(
        mixed, dpre, (((0,), (0,)), ((), ())), precision=highest, preferred_element_type=jnp.float32
    )
    local_time = jnp.sum(fraction[:, None] * dpre, axis=0)
    grad_in, grad_out = one_scatter((local_in, local_out), "row", (0, 1))
    grad_time, squared_all = packed_total((local_time, squared), "row")
    mse = squared_all / (noise_count * width)
    return (targets, row_pot, col_pot, grad_in, grad_time, grad_out, mse)


def solution(mesh):
    torus = Mesh(
        mesh.devices.reshape(mesh.shape["row"], 4, 2, 2), ("row", "col_0", "col_1", "col_2")
    )
    placed = (P("row", COL), P(COL, "row"), P("row"), P(None, COL), P(COL), P(COL, None))
    return jax.shard_map(
        body,
        mesh=torus,
        in_specs=placed,
        out_specs=(P("row", COL), P("row"), P(COL), P("row", COL), P(COL), P(COL, "row"), P()),
        check_vma=False,
    )
```

profile of v0, /device:TPU:0, one launch (start us, length us, event | category | flops | bytes accessed | tf_op | source)
XLA Modules:
  0.0 713.9 jit_solution(2502960895953794849)
XLA Ops:
  7.2 0.7 all-gather.5.cloned.1.call-update
  8.0 0.7 all-gather.7.cloned.1.call-update
  8.7 45.9 %all-gather.5.cloned.1.call-done = f32[512,3072]{0,1:T(8,128)} async-done(((f32[512,192]{0,1:T(8,128)}), f32[512,3072]{0,1:T(8,128)}) %all-gather.5.cloned.1.call-update) | async-done | bytes 6291472 | tf_op jit(solution)/shard_map/all_gather | solution.py:135
  54.6 3.3 multiply_reduce_fusion.1
  57.9 116.8 %all-gather.7.cloned.1.call-done = f32[768,3072]{1,0:T(8,128)} async-done(((f32[768,384]{1,0:T(8,128)}), f32[768,3072]{1,0:T(8,128)}) %all-gather.7.cloned.1.call-update) | async-done | bytes 9437200 | tf_op jit(solution)/shard_map/all_gather | solution.py:136
  174.7 4.5 multiply_reduce_fusion
  179.2 1.0 copy-done.6
  180.1 32.9 %subtract_reduce_fusion.3 = (f32[512]{0:T(512)S(1)}, f32[512,768]{1,0:T(8,128)S(1)}) fusion(f32[512,3072]{0,1:T(8,128)S(1)} %copy-done.6, f32[768,3072]{1,0:T(8,128)} %all-gather.7.cloned.1.call-done, f32[768]{0:T(1024)S(1)} %multiply_reduce_fusion, f32[512]{0:T(512)S(1)} %multiply_reduce_fusion.1), kind=kOutput, calls=%fused_computation.18 | convolution fusion | flops 14497873920 | bytes 17308672 | tf_op jit(solution)/shard_map/dot_general | solution.py:142
  213.0 1.2 copy-done.1
  214.2 0.4 exponential_reduce_fusion.4
  214.7 10.6 %all_to_all.37 = f32[16,2,512]{2,1,0:T(2,128)S(1)} all-to-all(f32[16,2,512]{2,1,0:T(2,128)S(1)} %broadcast_in_dim.14), channel_id=1, replica_groups=mesh['row'=8,'col_0'=4,'col_1'=2,'col_2'=2] {'col_0','col_1','col_2'}, dimensions={0} | all-to-all | bytes 131072 | tf_op jit(solution)/shard_map/all_to_all | solution.py:17
  225.7 1.7 subtract_reduce_fusion.2
  227.9 11.7 %all_to_all.38 = f32[8,2,768]{2,1,0:T(2,128)S(1)} all-to-all(f32[8,2,768]{2,1,0:T(2,128)S(1)} %broadcast_in_dim.15), channel_id=1, replica_groups=mesh['row'=8,'col_0'=4,'col_1'=2,'col_2'=2] {'row'}, dimensions={0} | all-to-all | bytes 98304 | tf_op jit(solution)/shard_map/all_to_all | solution.py:17
  240.0 1.7 subtract_reduce_fusion.1
  241.8 0.4 exponential_reduce_fusion.2
  242.2 8.7 %all_to_all.39 = f32[16,2,512]{2,1,0:T(2,128)S(1)} all-to-all(f32[16,2,512]{2,1,0:T(2,128)S(1)} %broadcast_in_dim.16), channel_id=1, replica_groups=mesh['row'=8,'col_0'=4,'col_1'=2,'col_2'=2] {'col_0','col_1','col_2'}, dimensions={0} | all-to-all | bytes 131072 | tf_op jit(solution)/shard_map/all_to_all | solution.py:17
  251.4 1.7 subtract_reduce_fusion
  253.6 10.2 %all_to_all.40 = f32[8,2,768]{2,1,0:T(2,128)S(1)} all-to-all(f32[8,2,768]{2,1,0:T(2,128)S(1)} %broadcast_in_dim.17), channel_id=1, replica_groups=mesh['row'=8,'col_0'=4,'col_1'=2,'col_2'=2] {'row'}, dimensions={0} | all-to-all | bytes 98304 | tf_op jit(solution)/shard_map/all_to_all | solution.py:17
  264.2 1.7 subtract_reduce_fusion.4
  266.4 8.7 %all_to_all.41 = f32[16,2,512]{2,1,0:T(2,128)S(1)} all-to-all(f32[16,2,512]{2,1,0:T(2,128)S(1)} %broadcast_in_dim.18), channel_id=1, replica_groups=mesh['row'=8,'col_0'=4,'col_1'=2,'col_2'=2] {'col_0','col_1','col_2'}, dimensions={0} | all-to-all | bytes 131072 | tf_op jit(solution)/shard_map/all_to_all | solution.py:17
  275.6 20.2 %fusion.2 = f32[512,3072]{0,1:T(8,128)} fusion(f32[768,3072]{1,0:T(8,128)} %all-gather.7.cloned.1.call-done, f32[512,768]{1,0:T(8,128)} %copy-done.1, f32[512]{0:T(512)S(1)} %bitcast.89, f32[768]{0:T(1024)S(1)} %subtract_reduce_fusion.5), kind=kOutput, calls=%fused_computation.6 | convolution fusion | flops 14496301056 | bytes 17306624 | tf_op jit(solution)/shard_map/dot_general | solution.py:160
  295.9 70.7 %reduce-scatter.5.cloned.1.call-done = f32[512,192]{0,1:T(8,128)} async-done(((f32[512,3072]{0,1:T(8,128)}), f32[512,192]{0,1:T(8,128)}) %reduce-scatter.5.cloned.1.call-update) | async-done | bytes 393232 | tf_op jit(solution)/shard_map/reduce_scatter | solution.py:165
  366.9 47.7 %all-gather.9.cloned.1.call-done = f32[512,3072]{0,1:T(8,128)} async-done(((f32[512,192]{0,1:T(8,128)}), f32[512,3072]{0,1:T(8,128)}) %all-gather.9.cloned.1.call-update) | async-done | bytes 6291472 | tf_op jit(solution)/shard_map/all_gather | solution.py:166
  414.6 9.0 %fusion.7 = f32[512,192]{0,1:T(8,128)S(1)} fusion(f32[3072,192]{0,1:T(8,128)} %param.9, f32[512,3072]{0,1:T(8,128)} %all-gather.9.cloned.1.call-done, f32[512,3072]{0,1:T(8,128)} %all-gather.5.cloned.1.call-done, f32[512]{0:T(512)S(1)} %get-tuple-element.76, f32[512]{0:T(512)S(1)} %get-tuple-element.75, f32[192]{0:T(256)S(1)} %copy-done.11), kind=kOutput, calls=%fused_computation.23 | convolution fusion | flops 3628793856 | bytes 15340288 | tf_op jit(solution)/shard_map/dot_general | solution.py:171
  423.5 5.6 fusion.14
  429.1 3.3 copy.49
  432.5 18.3 %reduce-scatter.7.cloned.1.call-done = f32[8,512,192]{1,2,0:T(8,128)} async-done(((f32[16,512,192]{1,2,0:T(8,128)}), f32[8,512,192]{1,2,0:T(8,128)}) %reduce-scatter.7.cloned.1.call-update) | async-done | bytes 3145744 | tf_op jit(solution)/shard_map/reduce_scatter | solution.py:79
  450.9 74.3 %reduce-scatter.9.cloned.1.call-done = f32[1,512,192]{1,2,0:T(8,128)} async-done(((f32[8,512,192]{1,2,0:T(8,128)}), f32[1,512,192]{1,2,0:T(8,128)}) %reduce-scatter.9.cloned.1.call-update) | async-done | bytes 393232 | tf_op jit(solution)/shard_map/reduce_scatter | solution.py:80
  525.2 2.0 multiply_reduce_fusion.2
  527.2 0.8 broadcast_multiply_fusion
  528.4 43.3 %all-gather.11.cloned.1.call-done = f32[512,3072]{0,1:T(8,128)} async-done(((f32[512,192]{0,1:T(8,128)}), f32[512,3072]{0,1:T(8,128)}) %all-gather.11.cloned.1.call-update) | async-done | bytes 6291472 | tf_op jit(solution)/shard_map/all_gather | solution.py:180
  571.7 7.1 multiply_reduce_fusion.3
  578.8 10.1 %fusion = f32[3072,192]{1,0:T(8,128)} fusion(f32[512,192]{0,1:T(8,128)S(1)} %get-tuple-element.80, f32[512,3072]{0,1:T(8,128)} %all-gather.9.cloned.1.call-done, f32[512,3072]{0,1:T(8,128)} %all-gather.5.cloned.1.call-done, f32[512]{0:T(512)S(1)} %get-tuple-element.76, f32[512]{0:T(512)S(1)} %get-tuple-element.75), kind=kOutput, calls=%fused_computation.4 | convolution fusion | flops 3628597248 | bytes 15339520 | tf_op jit(solution)/shard_map/dot_general | solution.py:196
  588.8 4.6 reshape_reshape.3
  593.4 8.6 %fusion.12 = f32[192,3072]{1,0:T(8,128)S(1)} fusion(f32[512,3072]{0,1:T(8,128)} %all-gather.11.cloned.1.call-done, f32[512,192]{0,1:T(8,128)S(1)} %fusion.7), kind=kOutput, calls=%fused_computation.33 | convolution fusion | flops 3624271872 | bytes 9043968 | tf_op jit(solution)/shard_map/dot_general | solution.py:181
  602.5 1.2 copy-done.7
  603.7 4.2 pad_maximum_fusion
  607.9 5.1 reshape.204
  613.1 0.7 broadcast_in_dim.19
  613.7 10.7 %all_to_all.42 = f32[16,1,1]{2,1,0:T(1,128)S(1)} all-to-all(f32[16,1,1]{2,1,0:T(1,128)S(1)} %broadcast_in_dim.19), channel_id=1, replica_groups=mesh['row'=8,'col_0'=4,'col_1'=2,'col_2'=2] {'col_0','col_1','col_2'}, dimensions={0} | all-to-all | bytes 128 | tf_op jit(solution)/shard_map/all_to_all | solution.py:17
  624.4 0.6 reduce_sum.108
  625.1 0.7 pad_maximum_fusion.6
  625.8 14.2 %all_to_all.43 = f32[8,1,193]{2,1,0:T(1,128)S(1)} all-to-all(f32[8,1,193]{2,1,0:T(1,128)S(1)} %broadcast_in_dim.20), channel_id=1, replica_groups=mesh['row'=8,'col_0'=4,'col_1'=2,'col_2'=2] {'row'}, dimensions={0} | all-to-all | bytes 12352 | tf_op jit(solution)/shard_map/all_to_all | solution.py:17
  640.0 0.6 slice.365
  641.2 61.4 %reduce-scatter.11.cloned.1.call-done = f32[1152,128]{1,0:T(8,128)} async-done(((f32[9216,128]{1,0:T(8,128)}), f32[1152,128]{1,0:T(8,128)}) %reduce-scatter.11.cloned.1.call-update) | async-done | bytes 589840 | tf_op jit(solution)/shard_map/reduce_scatter | solution.py:94
  702.6 1.1 fusion.29
  703.8 0.9 copy.53
  704.7 0.8 reshape.207
  (143 shorter events, 5.0 us)
Async XLA Ops:
  7.2 416.4 %copy-start = (f32[192,3072]{1,0:T(8,128)S(1)}, f32[192,3072]{1,0:T(8,128)}, u32[]{:S(2)}) copy-start(f32[192,3072]{1,0:T(8,128)} %param.11) | copy-start | bytes 7077892
  7.2 47.4 %all-gather.5.cloned.1.call-start = ((), (), s32[]{:S(2)}) async-start(), calls=%async_computation.11 | async-start | bytes 6684672 | tf_op jit(solution)/shard_map/all_gather | solution.py:135
  7.9 166.8 %all-gather.7.cloned.1.call-start = ((), (), s32[]{:S(2)}) async-start(), calls=%async_computation.12 | async-start | bytes 10616832 | tf_op jit(solution)/shard_map/all_gather | solution.py:136
  8.7 357.9 %reduce-scatter.5.cloned.1.call-start = ((), (), s32[]{:S(2)}) async-start(), calls=%async_computation.13 | async-start | bytes 6684672 | tf_op jit(solution)/shard_map/reduce_scatter | solution.py:165
  174.7 5.5 copy-start.6
  213.0 1.2 copy-start.1
  225.6 1.9 copy-start.2
  239.9 1.9 copy-start.3
  251.3 1.9 copy-start.4
  251.4 14.5 %copy-start.9 = (f32[1,512]{1,0:T(1,128)}, f32[1,512]{1,0:T(1,128)S(1)}, u32[]{:S(2)}) copy-start(f32[1,512]{1,0:T(1,128)S(1)} %add_subtract_fusion) | copy-start | bytes 6148
  264.1 1.9 copy-start.5
  264.2 31.7 %copy-start.8 = (f32[768]{0:T(1024)}, f32[768]{0:T(1024)S(1)}, u32[]{:S(2)}) copy-start(f32[768]{0:T(1024)S(1)} %subtract_reduce_fusion.5) | copy-start | bytes 9220
  295.8 71.0 %copy-start.10 = (s32[512]{0:T(512)S(1)}, s32[512]{0:T(512)}, u32[]{:S(2)}) copy-start(s32[512]{0:T(512)} %param.8) | copy-start | bytes 6148
  295.8 118.7 %copy-start.11 = (f32[192]{0:T(256)S(1)}, f32[192]{0:T(256)}, u32[]{:S(2)}) copy-start(f32[192]{0:T(256)} %param.10) | copy-start | bytes 2308
  295.9 118.7 %all-gather.9.cloned.1.call-start = ((), (), s32[]{:S(2)}) async-start(), calls=%async_computation.14 | async-start | bytes 6684672 | tf_op jit(solution)/shard_map/all_gather | solution.py:166
  366.6 84.3 %reduce-scatter.7.cloned.1.call-start = ((), (), s32[]{:S(2)}) async-start(), calls=%async_computation.15 | async-start | bytes 9437184 | tf_op jit(solution)/shard_map/reduce_scatter | solution.py:79
  432.5 92.8 %reduce-scatter.9.cloned.1.call-start = ((), (), s32[]{:S(2)}) async-start(), calls=%async_computation.16 | async-start | bytes 3538944 | tf_op jit(solution)/shard_map/reduce_scatter | solution.py:80
  450.9 120.8 %all-gather.11.cloned.1.call-start = ((), (), s32[]{:S(2)}) async-start(), calls=%async_computation.17 | async-start | bytes 6684672 | tf_op jit(solution)/shard_map/all_gather | solution.py:180
  528.1 174.6 %reduce-scatter.11.cloned.1.call-start = ((), (), s32[]{:S(2)}) async-start(), calls=%async_computation.18 | async-start | bytes 5308416 | tf_op jit(solution)/shard_map/reduce_scatter | solution.py:94
  602.0 1.7 copy-start.7
  640.0 65.5 %copy-start.12 = (f32[193]{0:T(256)}, f32[193]{0:T(256)S(1)}, u32[]{:S(2)}) copy-start(f32[193]{0:T(256)S(1)} %reduce_sum.109) | copy-start | bytes 2320
Sparse Core Ops, SparseCore 0:
  9.7 44.8 all-gather.4
  56.9 117.6 all-gather.6
  296.0 70.5 reduce-scatter.4
  368.7 45.8 all-gather.8
  432.6 18.2 reduce-scatter.6
  453.1 72.0 reduce-scatter.8
  528.2 43.4 all-gather.10
  613.2 89.3 reduce-scatter.10
where the time goes:
time: 723 us; the launch traced here: 714 us
  waiting for transfers between devices  480 us (66%)
  matrix products  93.4 us (13%)
  blocking collectives  74.7 us (10%)
  other arithmetic  25.3 us (3%)
  local copies, waits for them, and re-layouts  23 us (3%)
  between operations  16.8 us (2%)
    all_gather x1, waiting for transfers between devices, body(): full_images = lax.all_gather(images, 'row', axis=1, tiled=True)  117 us
    all_to_all x7, blocking collectives, sent_to_all(): lax.all_to_all(jnp.broadcast_to(array[None], (devices, *array.shape)), ax...  74.7 us
    reduce_scatter x1, waiting for transfers between devices, scatter_pairs(): return lax.psum_scatter(tiles, chips, scatter_dimension=0, tiled=True)[0]  74.3 us
    reduce_scatter x1, waiting for transfers between devices, body(): lax.psum_scatter(partial_value, COL, scatter_dimension=1, tiled=True)  70.7 us
    reduce_scatter x1, waiting for transfers between devices, one_scatter(): lax.psum_scatter(lines, axis, tiled=True).reshape(-1)  61.4 us
    all_gather x1, waiting for transfers between devices, body(): whole_targets = lax.all_gather(targets, COL, axis=1, tiled=True)  47.7 us
    all_gather x1, waiting for transfers between devices, body(): full_noise = lax.all_gather(noise, COL, axis=1, tiled=True)  45.9 us
    all_gather x1, waiting for transfers between devices, body(): lax.all_gather(diff_share / jnp.sqrt(jnp.float32(noise_count)), COL, axis...  43.3 us
  transfers between devices with their start and end apart: 8, of which 8 were waited for; matrix products, arithmetic and copies ran while one was open for 1% of the time, Pallas kernels for 0%

commit v1 on v0

v1 whole, which is shorter than its diff:
```python
import jax
import jax.numpy as jnp
from jax import lax
from jax.sharding import Mesh
from jax.sharding import PartitionSpec as P


ITERS = 2
TIMES = 1000
ROW = ("zh", "y")
COL = ("x", "zl", "c")
EPSILON = 0.01
PRECISION = lax.Precision.HIGH


def dot(a, b, ca, cb):
    return lax.dot_general(
        a,
        b,
        (((ca,), (cb,)), ((), ())),
        precision=PRECISION,
        preferred_element_type=jnp.float32,
    )


def moved(array, steps):
    axes = tuple(steps)
    sizes = [lax.axis_size(axis) for axis in axes]
    total = 1
    for size in sizes:
        total *= size
    pairs = []
    for source in range(total):
        rest, place, weight = source, 0, 1
        for axis, size in zip(reversed(axes), reversed(sizes)):
            place += (rest % size + steps[axis]) % size * weight
            weight, rest = weight * size, rest // size
        pairs.append((source, place))
    return lax.ppermute(array, axes if len(axes) > 1 else axes[0], pairs)


def around(array, ring, pair, far_by_pair=False):
    half = array.shape[0] // 2
    far = moved(array, {pair: 1})
    got = {(0, 0): array, (0, 1): far}
    for flip, own in ((0, array), (1, far)):
        got[1, flip] = moved(own, {ring: 1})
        got[3, flip] = moved(own, {ring: -1})
        if not far_by_pair:
            near = (3, -1) if flip else (1, 1)
            got[2, flip] = moved(got[near[0], flip], {ring: near[1]})
        elif flip:
            got[2, 1] = moved(got[2, 0], {pair: 1})
        else:
            right = moved(got[1, 0][:half], {ring: 1})
            left = moved(got[3, 0][half:], {ring: -1})
            got[2, 0] = jnp.concatenate([right, left])
    return got


def placed(got, ring, pair):
    buffer = jnp.zeros((8, *got[0, 0].shape), got[0, 0].dtype)
    here, side = lax.axis_index(ring), lax.axis_index(pair)
    for (step, flip), chunk in got.items():
        place = (here - step) % 4 * 2 + (side + flip) % 2
        buffer = lax.dynamic_update_index_in_dim(buffer, chunk, place, 0)
    return buffer


def gathered(chunk):
    return placed(around(chunk, "x", "zl"), "x", "zl").reshape(-1, chunk.shape[1])


def scattered(parts, ring, pair):
    right = moved(parts[2][0], {ring: 1})
    left = moved(parts[2][1], {ring: -1})
    a1 = moved(parts[1][1], {ring: 1})
    b0 = moved(parts[3][0], {ring: -1})
    a0 = moved(parts[1][0] + right, {ring: 1})
    b1 = moved(parts[3][1] + left, {ring: -1})
    second = [[a0, a1], [b0, b1]]
    mine = [parts[0][k] + second[0][k] + second[1][k] for k in (0, 1)]
    first = lax.axis_index(pair) == 0
    keep = jnp.where(first, mine[0], mine[1])
    send = jnp.where(first, mine[1], mine[0])
    return keep + moved(send, {pair: 1})


def both_cores(array, dim=0):
    other = moved(array, {"c": 1})
    first = lax.axis_index("c") == 0
    return jnp.concatenate([jnp.where(first, array, other), jnp.where(first, other, array)], dim)


def own_half(array, dim):
    low, high = jnp.split(array, 2, dim)
    first = lax.axis_index("c") == 0
    return jnp.where(first, low, high), jnp.where(first, high, low)


def turned(array, dim):
    own, other = own_half(array, dim)
    return jnp.concatenate([own, other], dim)


def joined(pieces):
    peaks = jnp.stack([piece[0] for piece in pieces])
    totals = jnp.stack([piece[1] for piece in pieces])
    peak = jnp.max(peaks, 0)
    return jnp.stack([peak, jnp.sum(totals * jnp.exp(peaks - peak), 0)])


def swapped(piece):
    low, high = jnp.split(piece, 2, 1)
    return jnp.concatenate([high, low], 1)


def over_images(logits):
    peak = jnp.max(logits, 0)
    both = jnp.stack([peak, jnp.sum(jnp.exp(logits - peak), 0)])
    both = joined(
        [
            both,
            moved(both, {"zl": 1}),
            swapped(moved(both, {"c": 1})),
            swapped(moved(both, {"zl": 1, "c": 1})),
        ]
    )
    both = joined([both] + [moved(both, {"x": step}) for step in (1, 2, 3)])
    return jnp.log(both[1]) + both[0]


def over_noise(logits):
    peak = jnp.max(logits, 1)
    both = jnp.stack([peak, jnp.sum(jnp.exp(logits - peak[:, None]), 1)])
    both = joined([both, moved(both, {"zh": 1})])
    both = joined([both] + [moved(both, {"y": step}) for step in (1, 2, 3)])
    return jnp.log(both[1]) + both[0]


def body(noise, images, time_index, w_in, time_gain, w_out):
    x, zl, c = (lax.axis_index(axis) for axis in COL)
    zh, y = (lax.axis_index(axis) for axis in ROW)
    width = noise.shape[1] * lax.axis_size(COL)
    noise_count = noise.shape[0] * lax.axis_size(ROW)
    image_count = images.shape[0] * lax.axis_size(COL)

    keep, send = own_half(noise.T, 1)
    got = moved(send, {"c": 1})
    own_noise = jnp.where(c == 0, jnp.concatenate([keep, got]), jnp.concatenate([got, keep]))
    half_noise = gathered(own_noise)
    full_noise = jnp.concatenate([half_noise, moved(half_noise, {"c": 1})], 1)
    depth = own_noise.shape[0]

    pieces = around(images, "y", "zh", True)
    image_at = jnp.stack([pieces[step, flip] for step in range(4) for flip in range(2)])
    cross, image_norms = 0.0, 0.0
    for step, flip in ((0, 0), (1, 0), (3, 0), (0, 1), (2, 0), (1, 1), (3, 1), (2, 1)):
        piece = pieces[step, flip]
        place = (zh + flip) % 2 * 4 + (y - step) % 4
        block = lax.dynamic_slice_in_dim(full_noise, place * depth, depth, 0)
        cross = lax.optimization_barrier(cross + dot(piece, block, 1, 0))
        image_norms = image_norms + jnp.sum(piece * piece, 1)
    noise_norms = jnp.sum(full_noise * full_noise, 0)
    scaled = (noise_norms[None, :] + image_norms[:, None] - 2.0 * cross) / (width * EPSILON)

    chip_in = both_cores(w_in.T)
    chip_out = both_cores(w_out)
    chip_gain = both_cores(time_gain)
    lines = jnp.zeros((4, w_out.shape[0], 2 * depth), w_out.dtype)
    for step in (0, 1, 3, 2):
        to = (x + step) % 4 * 2
        block = lax.dynamic_slice_in_dim(w_out, to * depth, 2 * depth, 1)
        if step:
            block = moved(block, {"x": step})
        lines = lax.dynamic_update_index_in_dim(lines, block, (x - step) % 4, 0)
    low, high = jnp.split(lines, 2, 2)
    keep = jnp.where(zl == 0, low, high)
    got = moved(jnp.where(zl == 0, high, low), {"zl": 1})
    columns = jnp.where(zl == 0, jnp.stack([keep, got], 1), jnp.stack([got, keep], 1))
    columns = both_cores(columns[:, :, None], 2).reshape(-1, depth)

    col_pot = jnp.zeros((images.shape[0],), jnp.float32)
    for _ in range(ITERS):
        row_pot = jnp.log(jnp.float32(image_count)) - over_images(col_pot[:, None] - scaled)
        col_pot = jnp.log(jnp.float32(noise_count)) - over_noise(row_pot[None, :] - scaled)
    logits = col_pot[:, None] - scaled
    weights = jnp.exp(logits - over_images(logits)[None, :])

    parts = {step: [None, None] for step in range(4)}
    for step, side in ((2, 0), (2, 1), (1, 1), (3, 0), (1, 0), (3, 1), (0, 0), (0, 1)):
        place = (x + step) % 4 * 2 + side
        place = (y - place) % 4 * 2 + (zh + place // 4) % 2
        block = lax.dynamic_index_in_dim(image_at, place, 0, False)
        part = dot(block, weights, 0, 0)
        own, other = jnp.split(part, 2, 1)
        parts[step][side] = own + moved(other, {"c": 1})
    own_targets = scattered(parts, "x", "zl")

    keep, send = own_half(own_targets, 0)
    targets = turned(jnp.concatenate([keep, moved(send, {"c": 1})], 1), 1).T

    fraction = (time_index.astype(jnp.float32) + 0.5) / TIMES
    fraction = own_half(fraction, 0)[0]
    mixed = (1.0 - fraction) * own_noise + fraction * own_targets
    all_mixed = gathered(mixed)
    pre = dot(chip_in, all_mixed, 1, 0) + chip_gain[:, None] * fraction
    sigma = jax.nn.sigmoid(pre)
    hidden = pre * sigma
    all_hidden = gathered(hidden)
    out = dot(columns, all_hidden, 0, 0)
    diff = out - (own_targets - own_noise)
    slope = diff / jnp.sqrt(jnp.float32(noise_count))
    all_slope = gathered(slope)
    squared = jnp.sum(all_slope * all_slope) * noise_count

    def whole(array):
        keep, send = own_half(array, 0)
        return jnp.concatenate([keep, moved(send, {"c": 1})], 1)

    def gradient(left, right):
        right = jnp.concatenate([right, moved(right, {"c": 1})], 1)
        parts = {step: [None, None] for step in range(4)}
        for step, side in ((2, 0), (2, 1), (1, 1), (3, 0), (1, 0), (3, 1), (0, 0), (0, 1)):
            place = side * 4 + (y + step) % 4
            block = lax.dynamic_slice_in_dim(right, place * depth, depth, 0)
            parts[step][side] = dot(left, block, 1, 1)
        return scattered(parts, "y", "zh")

    grad_out = gradient(whole(hidden), all_slope)
    back = dot(chip_out, all_slope, 1, 0)
    dpre = back * sigma * (1.0 + pre * (1.0 - sigma))
    grad_in = gradient(whole(dpre), all_mixed).T

    sums = jnp.concatenate([jnp.sum(fraction * dpre, 1), squared[None]])
    sums = jnp.pad(sums, (0, -len(sums) % 128))
    sums = sums + moved(sums, {"c": 1})
    sums = sums + moved(sums, {"zh": 1})
    sums = sums + (moved(sums, {"y": 1}) + moved(sums, {"y": 2}) + moved(sums, {"y": 3}))
    grad_time = own_half(sums[: 2 * w_in.shape[1]], 0)[0]
    mse = sums[2 * w_in.shape[1]] / (noise_count * width)
    return (targets, turned(row_pot, 0), col_pot, grad_in, grad_time, grad_out, mse)


def solution(mesh):
    torus = Mesh(mesh.devices.reshape(2, 4, 4, 2, 2), (*ROW, *COL))
    return jax.shard_map(
        body,
        mesh=torus,
        in_specs=(P(ROW, COL), P(COL, ROW), P(ROW), P(None, COL), P(COL), P(COL, None)),
        out_specs=(P(ROW, COL), P(ROW), P(COL), P(ROW, COL), P(COL), P(COL, ROW), P()),
        check_vma=False,
    )
```

time: 723 us -> 476 us (0.66)
  the two profiles are of different devices: /device:TPU:0 before, /device:TPU:6 now
where the time goes in v1:
time: 476 us; the launch traced here: 467 us
  waiting for transfers between devices  197 us (41%)
  starting transfers between devices  113 us (24%)
  matrix products  83.4 us (18%)
  local copies, waits for them, and re-layouts  36.6 us (8%)
  other arithmetic  31.8 us (7%)
  between operations  5.05 us (1%)
    ppermute x111, waiting for transfers between devices, moved(): return lax.ppermute(array, axes if len(axes) > 1 else axes[0], pairs)  197 us
    ppermute x111, starting transfers between devices, moved(): return lax.ppermute(array, axes if len(axes) > 1 else axes[0], pairs)  113 us
    dot_general x35, matrix products, dot(): lax.dot_general(a, b, (((ca,), (cb,)), ((), ())), precision=PRECISION, pr...  83.4 us
  transfers between devices with their start and end apart: 111, of which 63 were waited for; matrix products, arithmetic and copies ran while one was open for 31% of the time, Pallas kernels for 0%

profile of v1, /device:TPU:6, one launch (start us, length us, event | category | flops | bytes accessed | tf_op | source)
XLA Modules:
  0.0 466.7 jit_solution(13279896775427328957)
XLA Ops:
  11.6 3.0 collective-permute-done.10
  18.7 2.6 collective-permute-done.11
  22.5 4.3 collective-permute-done.12
  26.8 3.9 collective-permute-start
  33.6 6.5 %collective-permute-done.15 = f32[384,256]{1,0:T(8,128)S(1)} collective-permute-done((f32[384,256]{1,0:T(8,128)S(1)}, f32[384,256]{1,0:T(8,128)S(1)}, u32[]{:S(2)}, u32[]{:S(2)}) %collective-permute-start.15) | collective-permute-done | bytes 393248 | tf_op jit(solution)/shard_map/ppermute | solution.py:39
  40.2 2.7 constant_dynamic-slice_fusion
  60.6 5.0 %collective-permute-done.3 = f32[384,384]{1,0:T(8,128)} collective-permute-done((f32[384,384]{1,0:T(8,128)}, f32[384,384]{1,0:T(8,128)}, u32[]{:S(2)}, u32[]{:S(2)}) %collective-permute-start.3) | collective-permute-done | bytes 589856 | tf_op jit(solution)/shard_map/ppermute | solution.py:39
  77.7 15.1 %collective-permute-done.7 = f32[768,384]{1,0:T(8,128)} collective-permute-done((f32[768,384]{1,0:T(8,128)}, f32[768,384]{1,0:T(8,128)}, u32[]{:S(2)}, u32[]{:S(2)}) %collective-permute-start.7) | collective-permute-done | bytes 1179680 | tf_op jit(solution)/shard_map/ppermute | solution.py:39
  96.4 3.2 collective-permute-done.6
  99.9 3.5 convolution_bitcast_fusion
  103.4 3.5 fusion.91
  107.1 3.5 fusion.94
  110.8 3.5 fusion.97
  114.5 2.5 fusion.100
  117.3 3.4 bitcast_add_fusion.1
  120.7 3.5 fusion.105
  124.4 2.5 fusion.108
  144.9 3.0 collective-permute-start.23
  151.9 3.6 collective-permute-start.25
  164.6 8.2 %collective-permute-done.29 = f32[2,512]{1,0:T(2,128)S(1)} collective-permute-done((f32[2,512]{1,0:T(2,128)S(1)}, f32[2,512]{1,0:T(2,128)S(1)}, u32[]{:S(2)}, u32[]{:S(2)}) %collective-permute-start.29) | collective-permute-done | bytes 4128 | tf_op jit(solution)/shard_map/ppermute | solution.py:39
  183.9 3.6 collective-permute-done.33
  189.2 3.6 collective-permute-start.35
  208.1 2.7 collective-permute-done.41
  234.8 3.2 collective-permute-start.46
  238.8 8.6 %collective-permute-done.55 = f32[384,256]{1,0:T(8,128)S(1)} collective-permute-done((f32[384,256]{1,0:T(8,128)S(1)}, f32[384,256]{1,0:T(8,128)S(1)}, u32[]{:S(2)}, u32[]{:S(2)}) %collective-permute-start.55) | collective-permute-done | bytes 393248 | tf_op jit(solution)/shard_map/ppermute | solution.py:39
  247.8 2.5 collective-permute-start.52
  250.7 8.6 %collective-permute-done.52 = f32[384,256]{1,0:T(8,128)S(1)} collective-permute-done((f32[384,256]{1,0:T(8,128)S(1)}, f32[384,256]{1,0:T(8,128)S(1)}, u32[]{:S(2)}, u32[]{:S(2)}) %collective-permute-start.52) | collective-permute-done | bytes 393248 | tf_op jit(solution)/shard_map/ppermute | solution.py:39
  263.8 6.4 %collective-permute-done.56 = f32[384,256]{1,0:T(8,128)S(1)} collective-permute-done((f32[384,256]{1,0:T(8,128)S(1)}, f32[384,256]{1,0:T(8,128)S(1)}, u32[]{:S(2)}, u32[]{:S(2)}) %collective-permute-start.56) | collective-permute-done | bytes 393248 | tf_op jit(solution)/shard_map/ppermute | solution.py:39
  272.7 7.3 %collective-permute-done.57 = f32[384,256]{1,0:T(8,128)S(1)} collective-permute-done((f32[384,256]{1,0:T(8,128)S(1)}, f32[384,256]{1,0:T(8,128)S(1)}, u32[]{:S(2)}, u32[]{:S(2)}) %collective-permute-start.57) | collective-permute-done | bytes 393248 | tf_op jit(solution)/shard_map/ppermute | solution.py:39
  285.7 2.7 broadcast_select_fusion.5
  301.7 4.4 collective-permute-done.71
  306.8 2.7 collective-permute-done.69
  312.0 3.1 collective-permute-done.72
  316.2 4.1 bitcast_dynamic-update-slice_fusion.27
  323.9 4.4 collective-permute-done.74
  330.3 2.6 collective-permute-done.75
  334.3 5.1 %collective-permute-done.79 = f32[384,256]{1,0:T(8,128)S(1)} collective-permute-done((f32[384,256]{1,0:T(8,128)S(1)}, f32[384,256]{1,0:T(8,128)S(1)}, u32[]{:S(2)}, u32[]{:S(2)}) %collective-permute-start.79) | collective-permute-done | bytes 393248 | tf_op jit(solution)/shard_map/ppermute | solution.py:39
  339.7 5.8 %collective-permute-done.77 = f32[384,256]{1,0:T(8,128)S(1)} collective-permute-done((f32[384,256]{1,0:T(8,128)S(1)}, f32[384,256]{1,0:T(8,128)S(1)}, u32[]{:S(2)}, u32[]{:S(2)}) %collective-permute-start.77) | collective-permute-done | bytes 393248 | tf_op jit(solution)/shard_map/ppermute | solution.py:39
  345.6 3.0 collective-permute-done.80
  348.9 4.0 bitcast_dynamic-update-slice_fusion.19
  357.8 6.7 %collective-permute-done.82 = f32[384,256]{1,0:T(8,128)S(1)} collective-permute-done((f32[384,256]{1,0:T(8,128)S(1)}, f32[384,256]{1,0:T(8,128)S(1)}, u32[]{:S(2)}, u32[]{:S(2)}) %collective-permute-start.82) | collective-permute-done | bytes 393248 | tf_op jit(solution)/shard_map/ppermute | solution.py:39
  369.0 7.5 %collective-permute-done.86 = f32[384,256]{1,0:T(8,128)S(1)} collective-permute-done((f32[384,256]{1,0:T(8,128)S(1)}, f32[384,256]{1,0:T(8,128)S(1)}, u32[]{:S(2)}, u32[]{:S(2)}) %collective-permute-start.86) | collective-permute-done | bytes 393248 | tf_op jit(solution)/shard_map/ppermute | solution.py:39
  377.4 3.3 collective-permute-done.85
  380.7 7.0 %collective-permute-done.87 = f32[384,256]{1,0:T(8,128)S(1)} collective-permute-done((f32[384,256]{1,0:T(8,128)S(1)}, f32[384,256]{1,0:T(8,128)S(1)}, u32[]{:S(2)}, u32[]{:S(2)}) %collective-permute-start.87) | collective-permute-done | bytes 393248 | tf_op jit(solution)/shard_map/ppermute | solution.py:39
  390.8 4.6 multiply_reduce_fusion.9
  397.7 4.2 collective-permute-done.98
  434.9 3.3 collective-permute-start.108
  446.7 2.9 collective-permute-start.109
  (418 shorter events, 246.6 us)
Async XLA Ops:
  3.7 12.5 %collective-permute-start.9 = (f32[384,256]{1,0:T(8,128)S(1)}, f32[384,256]{1,0:T(8,128)}, u32[]{:S(2)}, u32[]{:S(2)}) collective-permute-start(f32[384,256]{1,0:T(8,128)S(1)} %maximum_select_fusion.2), channel_id=1, source_target_pairs={{0,2},{2,0},{1,3},{3,1},{4,6},{6,4},{5,7},{7,5},{8,10},{10,8},{9,1... | collective-permute-start | bytes 1179656 | tf_op jit(solution)/shard_map/ppermute | solution.py:39
  5.7 40.9 %collective-permute-start.1 = (f32[768,384]{1,0:T(8,128)}, f32[768,384]{1,0:T(8,128)}, u32[]{:S(2)}, u32[]{:S(2)}) collective-permute-start(f32[768,384]{1,0:T(8,128)} %param.7), channel_id=1, source_target_pairs={{0,16},{16,32},{32,48},{48,0},{1,17},{17,33},{33,49},{49,1},{2,18}... | collective-permute-start | bytes 3538952 | tf_op jit(solution)/shard_map/ppermute | solution.py:39
  7.3 42.8 %collective-permute-start.4 = (f32[768,384]{1,0:T(8,128)}, f32[768,384]{1,0:T(8,128)}, u32[]{:S(2)}, u32[]{:S(2)}) collective-permute-start(f32[768,384]{1,0:T(8,128)} %param.7), channel_id=1, source_target_pairs={{0,48},{16,0},{32,16},{48,32},{1,49},{17,1},{33,17},{49,33},{2,50}... | collective-permute-start | bytes 3538952 | tf_op jit(solution)/shard_map/ppermute | solution.py:39
  9.0 12.4 %collective-permute-start.11 = (f32[384,256]{1,0:T(8,128)S(1)}, f32[384,256]{1,0:T(8,128)S(1)}, u32[]{:S(2)}, u32[]{:S(2)}) collective-permute-start(f32[384,256]{1,0:T(8,128)S(1)} %maximum_select_fusion.2), channel_id=1, source_target_pairs={{0,12},{4,0},{8,4},{12,8},{1,13},{5,1},{9,5},{13,9},{2,14},{6,2},{... | collective-permute-start | bytes 1179656 | tf_op jit(solution)/shard_map/ppermute | solution.py:39
  14.6 12.2 %collective-permute-start.12 = (f32[384,256]{1,0:T(8,128)}, f32[384,256]{1,0:T(8,128)S(1)}, u32[]{:S(2)}, u32[]{:S(2)}) collective-permute-start(f32[384,256]{1,0:T(8,128)} %collective-permute-done.10), channel_id=1, source_target_pairs={{0,4},{4,8},{8,12},{12,0},{1,5},{5,9},{9,13},{13,1},{2,6},{6,10},{... | collective-permute-start | bytes 1179656 | tf_op jit(solution)/shard_map/ppermute | solution.py:39
  16.2 14.5 %collective-permute-start.14 = (f32[384,256]{1,0:T(8,128)}, f32[384,256]{1,0:T(8,128)S(1)}, u32[]{:S(2)}, u32[]{:S(2)}) collective-permute-start(f32[384,256]{1,0:T(8,128)} %collective-permute-done.9), channel_id=1, source_target_pairs={{0,12},{4,0},{8,4},{12,8},{1,13},{5,1},{9,5},{13,9},{2,14},{6,2},{... | collective-permute-start | bytes 1179656 | tf_op jit(solution)/shard_map/ppermute | solution.py:39
  21.4 12.2 %collective-permute-start.13 = (f32[384,256]{1,0:T(8,128)}, f32[384,256]{1,0:T(8,128)S(1)}, u32[]{:S(2)}, u32[]{:S(2)}) collective-permute-start(f32[384,256]{1,0:T(8,128)} %collective-permute-done.9), channel_id=1, source_target_pairs={{0,4},{4,8},{8,12},{12,0},{1,5},{5,9},{9,13},{13,1},{2,6},{6,10},{... | collective-permute-start | bytes 1179656 | tf_op jit(solution)/shard_map/ppermute | solution.py:39
  26.8 28.4 %collective-permute-start = (f32[768,384]{1,0:T(8,128)}, f32[768,384]{1,0:T(8,128)}, u32[]{:S(2)}, u32[]{:S(2)}) collective-permute-start(f32[768,384]{1,0:T(8,128)} %param.7), channel_id=1, source_target_pairs={{0,64},{64,0},{1,65},{65,1},{2,66},{66,2},{3,67},{67,3},{4,68},{68... | collective-permute-start | bytes 3538952 | tf_op jit(solution)/shard_map/ppermute | solution.py:39
  40.1 59.8 %collective-permute-start.16 = (f32[3072,256]{1,0:T(8,128)S(1)}, f32[3072,256]{1,0:T(8,128)}, u32[]{:S(2)}, u32[]{:S(2)}) collective-permute-start(f32[3072,256]{1,0:T(8,128)S(1)} %bitcast.188), channel_id=1, source_target_pairs={{0,1},{1,0},{2,3},{3,2},{4,5},{5,4},{6,7},{7,6},{8,9},{9,8},{10,11... | collective-permute-start | bytes 9437192 | tf_op jit(solution)/shard_map/ppermute | solution.py:39
  43.0 26.7 %collective-permute-start.60 = (f32[192,768]{1,0:T(8,128)}, f32[192,768]{1,0:T(8,128)}, u32[]{:S(2)}, u32[]{:S(2)}) collective-permute-start(f32[192,768]{1,0:T(8,128)} %get-tuple-element.45), channel_id=1, source_target_pairs={{0,4},{4,8},{8,12},{12,0},{1,5},{5,9},{9,13},{13,1},{2,6},{6,10},{... | collective-permute-start | bytes 1769480 | tf_op jit(solution)/shard_map/ppermute | solution.py:39
  48.6 17.0 %collective-permute-start.3 = (f32[384,384]{1,0:T(8,128)}, f32[384,384]{1,0:T(8,128)}, u32[]{:S(2)}, u32[]{:S(2)}) collective-permute-start(f32[384,384]{1,0:T(8,128)} %slice.223), channel_id=1, source_target_pairs={{0,16},{16,32},{32,48},{48,0},{1,17},{17,33},{33,49},{49,1},{2,18}... | collective-permute-start | bytes 1769480 | tf_op jit(solution)/shard_map/ppermute | solution.py:39
  52.1 16.5 %collective-permute-start.5 = (f32[384,384]{1,0:T(8,128)}, f32[384,384]{1,0:T(8,128)}, u32[]{:S(2)}, u32[]{:S(2)}) collective-permute-start(f32[384,384]{1,0:T(8,128)} %slice.224), channel_id=1, source_target_pairs={{0,48},{16,0},{32,16},{48,32},{1,49},{17,1},{33,17},{49,33},{2,50}... | collective-permute-start | bytes 1769480 | tf_op jit(solution)/shard_map/ppermute | solution.py:39
  55.2 37.6 %collective-permute-start.7 = (f32[768,384]{1,0:T(8,128)}, f32[768,384]{1,0:T(8,128)}, u32[]{:S(2)}, u32[]{:S(2)}) collective-permute-start(f32[768,384]{1,0:T(8,128)} %collective-permute-done), channel_id=1, source_target_pairs={{0,48},{16,0},{32,16},{48,32},{1,49},{17,1},{33,17},{49,33},{2,50}... | collective-permute-start | bytes 3538952 | tf_op jit(solution)/shard_map/ppermute | solution.py:39
  65.5 29.0 %collective-permute-start.2 = (f32[768,384]{1,0:T(8,128)}, f32[768,384]{1,0:T(8,128)S(1)}, u32[]{:S(2)}, u32[]{:S(2)}) collective-permute-start(f32[768,384]{1,0:T(8,128)} %collective-permute-done), channel_id=1, source_target_pairs={{0,16},{16,32},{32,48},{48,0},{1,17},{17,33},{33,49},{49,1},{2,18}... | collective-permute-start | bytes 3538952 | tf_op jit(solution)/shard_map/ppermute | solution.py:39
  68.6 203.6 %collective-permute-start.65 = (f32[192,3072]{1,0:T(8,128)}, f32[192,3072]{1,0:T(8,128)S(1)}, u32[]{:S(2)}, u32[]{:S(2)}) collective-permute-start(f32[192,3072]{1,0:T(8,128)} %bitcast.202), channel_id=1, source_target_pairs={{0,1},{1,0},{2,3},{3,2},{4,5},{5,4},{6,7},{7,6},{8,9},{9,8},{10,11... | collective-permute-start | bytes 7077896 | tf_op jit(solution)/shard_map/ppermute | solution.py:39
  69.7 30.0 %collective-permute-start.6 = (f32[768,384]{1,0:T(8,128)S(1)}, f32[768,384]{1,0:T(8,128)S(1)}, u32[]{:S(2)}, u32[]{:S(2)}) collective-permute-start(f32[768,384]{1,0:T(8,128)S(1)} %constant_dynamic-update-slice_fusion), channel_id=1, source_target_pairs={{0,64},{64,0},{1,65},{65,1},{2,66},{66,2},{3,67},{67,3},{4,68},{68... | collective-permute-start | bytes 3538952 | tf_op jit(solution)/shard_map/ppermute | solution.py:39
  92.8 38.1 %collective-permute-start.61 = (f32[192,768]{1,0:T(8,128)S(1)}, f32[192,768]{1,0:T(8,128)S(1)}, u32[]{:S(2)}, u32[]{:S(2)}) collective-permute-start(f32[192,768]{1,0:T(8,128)S(1)} %copy-done.11), channel_id=1, source_target_pairs={{0,12},{4,0},{8,4},{12,8},{1,13},{5,1},{9,5},{13,9},{2,14},{6,2},{... | collective-permute-start | bytes 1769480 | tf_op jit(solution)/shard_map/ppermute | solution.py:39
  94.6 44.4 %collective-permute-start.62 = (f32[192,768]{1,0:T(8,128)S(1)}, f32[192,768]{1,0:T(8,128)S(1)}, u32[]{:S(2)}, u32[]{:S(2)}) collective-permute-start(f32[192,768]{1,0:T(8,128)S(1)} %copy-done.10), channel_id=1, source_target_pairs={{0,8},{4,12},{8,0},{12,4},{1,9},{5,13},{9,1},{13,5},{2,10},{6,14},... | collective-permute-start | bytes 1769480 | tf_op jit(solution)/shard_map/ppermute | solution.py:39
  149.7 84.9 %collective-permute-start.63 = (f32[4,192,384]{2,1,0:T(8,128)S(1)}, f32[4,192,384]{2,1,0:T(8,128)S(1)}, u32[]{:S(2)}, u32[]{:S(2)}) collective-permute-start(f32[4,192,384]{2,1,0:T(8,128)S(1)} %get-tuple-element.43), channel_id=1, source_target_pairs={{0,2},{2,0},{1,3},{3,1},{4,6},{6,4},{5,7},{7,5},{8,10},{10,8},{9,1... | collective-permute-start | bytes 3538952 | tf_op jit(solution)/shard_map/ppermute | solution.py:39
  160.9 11.8 %collective-permute-start.29 = (f32[2,512]{1,0:T(2,128)S(1)}, f32[2,512]{1,0:T(2,128)S(1)}, u32[]{:S(2)}, u32[]{:S(2)}) collective-permute-start(f32[2,512]{1,0:T(2,128)S(1)} %pad_maximum_fusion.12), channel_id=1, source_target_pairs={{0,3},{1,2},{2,1},{3,0},{4,7},{5,6},{6,5},{7,4},{8,11},{9,10},{10,... | collective-permute-start | bytes 12296 | tf_op jit(solution)/shard_map/ppermute | solution.py:39
  216.5 18.3 %collective-permute-start.51 = (f32[384,256]{1,0:T(8,128)S(1)}, f32[384,256]{1,0:T(8,128)S(1)}, u32[]{:S(2)}, u32[]{:S(2)}) collective-permute-start(f32[384,256]{1,0:T(8,128)S(1)} %split.201), channel_id=1, source_target_pairs={{0,1},{1,0},{2,3},{3,2},{4,5},{5,4},{6,7},{7,6},{8,9},{9,8},{10,11... | collective-permute-start | bytes 1179656 | tf_op jit(solution)/shard_map/ppermute | solution.py:39
  234.8 12.6 %collective-permute-start.55 = (f32[384,256]{1,0:T(8,128)S(1)}, f32[384,256]{1,0:T(8,128)S(1)}, u32[]{:S(2)}, u32[]{:S(2)}) collective-permute-start(f32[384,256]{1,0:T(8,128)S(1)} %slice_add_fusion), channel_id=1, source_target_pairs={{0,12},{4,0},{8,4},{12,8},{1,13},{5,1},{9,5},{13,9},{2,14},{6,2},{... | collective-permute-start | bytes 1179656 | tf_op jit(solution)/shard_map/ppermute | solution.py:39
  234.8 13.1 %collective-permute-start.46 = (f32[384,256]{1,0:T(8,128)S(1)}, f32[384,256]{1,0:T(8,128)S(1)}, u32[]{:S(2)}, u32[]{:S(2)}) collective-permute-start(f32[384,256]{1,0:T(8,128)S(1)} %slice_add_fusion.5), channel_id=1, source_target_pairs={{0,4},{4,8},{8,12},{12,0},{1,5},{5,9},{9,13},{13,1},{2,6},{6,10},{... | collective-permute-start | bytes 1179656 | tf_op jit(solution)/shard_map/ppermute | solution.py:39
  238.2 47.6 %collective-permute-start.59 = (f32[192,3072]{1,0:T(8,128)S(1)}, f32[192,3072]{1,0:T(8,128)S(1)}, u32[]{:S(2)}, u32[]{:S(2)}) collective-permute-start(f32[192,3072]{1,0:T(8,128)S(1)} %copy-done), channel_id=1, source_target_pairs={{0,1},{1,0},{2,3},{3,2},{4,5},{5,4},{6,7},{7,6},{8,9},{9,8},{10,11... | collective-permute-start | bytes 7077896 | tf_op jit(solution)/shard_map/ppermute | solution.py:39
  238.3 12.3 %collective-permute-start.50 = (f32[384,256]{1,0:T(8,128)S(1)}, f32[384,256]{1,0:T(8,128)S(1)}, u32[]{:S(2)}, u32[]{:S(2)}) collective-permute-start(f32[384,256]{1,0:T(8,128)S(1)} %split.199), channel_id=1, source_target_pairs={{0,1},{1,0},{2,3},{3,2},{4,5},{5,4},{6,7},{7,6},{8,9},{9,8},{10,11... | collective-permute-start | bytes 1179656 | tf_op jit(solution)/shard_map/ppermute | solution.py:39
  250.5 13.3 %collective-permute-start.49 = (f32[384,256]{1,0:T(8,128)S(1)}, f32[384,256]{1,0:T(8,128)S(1)}, u32[]{:S(2)}, u32[]{:S(2)}) collective-permute-start(f32[384,256]{1,0:T(8,128)S(1)} %slice_add_fusion.4), channel_id=1, source_target_pairs={{0,12},{4,0},{8,4},{12,8},{1,13},{5,1},{9,5},{13,9},{2,14},{6,2},{... | collective-permute-start | bytes 1179656 | tf_op jit(solution)/shard_map/ppermute | solution.py:39
  250.6 19.6 %collective-permute-start.56 = (f32[384,256]{1,0:T(8,128)S(1)}, f32[384,256]{1,0:T(8,128)S(1)}, u32[]{:S(2)}, u32[]{:S(2)}) collective-permute-start(f32[384,256]{1,0:T(8,128)S(1)} %fusion.110), channel_id=1, source_target_pairs={{0,12},{4,0},{8,4},{12,8},{1,13},{5,1},{9,5},{13,9},{2,14},{6,2},{... | collective-permute-start | bytes 1179656 | tf_op jit(solution)/shard_map/ppermute | solution.py:39
  263.8 57.2 %collective-permute-start.64 = (f32[4,2,1,192,384]{4,3,2,1,0:T(8,128)S(1)}, f32[4,2,1,192,384]{4,3,2,1,0:T(8,128)S(1)}, u32[]{:S(2)}, u32[]{:S(2)}) collective-permute-start(f32[4,2,1,192,384]{4,3,2,1,0:T(8,128)S(1)} %maximum_select_fusion), channel_id=1, source_target_pairs={{0,1},{1,0},{2,3},{3,2},{4,5},{5,4},{6,7},{7,6},{8,9},{9,8},{10,11... | collective-permute-start | bytes 7077896 | tf_op jit(solution)/shard_map/ppermute | solution.py:39
  288.4 12.6 %collective-permute-start.68 = (f32[384,256]{1,0:T(8,128)S(1)}, f32[384,256]{1,0:T(8,128)S(1)}, u32[]{:S(2)}, u32[]{:S(2)}) collective-permute-start(f32[384,256]{1,0:T(8,128)S(1)} %get-tuple-element.16), channel_id=1, source_target_pairs={{0,12},{4,0},{8,4},{12,8},{1,13},{5,1},{9,5},{13,9},{2,14},{6,2},{... | collective-permute-start | bytes 1179656 | tf_op jit(solution)/shard_map/ppermute | solution.py:39
  291.5 18.9 %collective-permute-start.70 = (f32[384,256]{1,0:T(8,128)S(1)}, f32[384,256]{1,0:T(8,128)S(1)}, u32[]{:S(2)}, u32[]{:S(2)}) collective-permute-start(f32[384,256]{1,0:T(8,128)S(1)} %collective-permute-done.66), channel_id=1, source_target_pairs={{0,4},{4,8},{8,12},{12,0},{1,5},{5,9},{9,13},{13,1},{2,6},{6,10},{... | collective-permute-start | bytes 1179656 | tf_op jit(solution)/shard_map/ppermute | solution.py:39
  292.0 14.1 %collective-permute-start.71 = (f32[384,256]{1,0:T(8,128)S(1)}, f32[384,256]{1,0:T(8,128)S(1)}, u32[]{:S(2)}, u32[]{:S(2)}) collective-permute-start(f32[384,256]{1,0:T(8,128)S(1)} %collective-permute-done.66), channel_id=1, source_target_pairs={{0,12},{4,0},{8,4},{12,8},{1,13},{5,1},{9,5},{13,9},{2,14},{6,2},{... | collective-permute-start | bytes 1179656 | tf_op jit(solution)/shard_map/ppermute | solution.py:39
  294.7 14.9 %collective-permute-start.69 = (f32[384,256]{1,0:T(8,128)S(1)}, f32[384,256]{1,0:T(8,128)S(1)}, u32[]{:S(2)}, u32[]{:S(2)}) collective-permute-start(f32[384,256]{1,0:T(8,128)S(1)} %collective-permute-done.67), channel_id=1, source_target_pairs={{0,4},{4,8},{8,12},{12,0},{1,5},{5,9},{9,13},{13,1},{2,6},{6,10},{... | collective-permute-start | bytes 1179656 | tf_op jit(solution)/shard_map/ppermute | solution.py:39
  320.9 12.0 %collective-permute-start.75 = (f32[384,256]{1,0:T(8,128)S(1)}, f32[384,256]{1,0:T(8,128)S(1)}, u32[]{:S(2)}, u32[]{:S(2)}) collective-permute-start(f32[384,256]{1,0:T(8,128)S(1)} %fusion.117), channel_id=1, source_target_pairs={{0,4},{4,8},{8,12},{12,0},{1,5},{5,9},{9,13},{13,1},{2,6},{6,10},{... | collective-permute-start | bytes 1179656 | tf_op jit(solution)/shard_map/ppermute | solution.py:39
  321.9 12.3 %collective-permute-start.76 = (f32[384,256]{1,0:T(8,128)S(1)}, f32[384,256]{1,0:T(8,128)S(1)}, u32[]{:S(2)}, u32[]{:S(2)}) collective-permute-start(f32[384,256]{1,0:T(8,128)S(1)} %fusion.117), channel_id=1, source_target_pairs={{0,12},{4,0},{8,4},{12,8},{1,13},{5,1},{9,5},{13,9},{2,14},{6,2},{... | collective-permute-start | bytes 1179656 | tf_op jit(solution)/shard_map/ppermute | solution.py:39
  328.3 17.3 %collective-permute-start.78 = (f32[384,256]{1,0:T(8,128)S(1)}, f32[384,256]{1,0:T(8,128)S(1)}, u32[]{:S(2)}, u32[]{:S(2)}) collective-permute-start(f32[384,256]{1,0:T(8,128)S(1)} %collective-permute-done.74), channel_id=1, source_target_pairs={{0,4},{4,8},{8,12},{12,0},{1,5},{5,9},{9,13},{13,1},{2,6},{6,10},{... | collective-permute-start | bytes 1179656 | tf_op jit(solution)/shard_map/ppermute | solution.py:39
  332.9 12.5 %collective-permute-start.77 = (f32[384,256]{1,0:T(8,128)S(1)}, f32[384,256]{1,0:T(8,128)S(1)}, u32[]{:S(2)}, u32[]{:S(2)}) collective-permute-start(f32[384,256]{1,0:T(8,128)S(1)} %collective-permute-done.75), channel_id=1, source_target_pairs={{0,4},{4,8},{8,12},{12,0},{1,5},{5,9},{9,13},{13,1},{2,6},{6,10},{... | collective-permute-start | bytes 1179656 | tf_op jit(solution)/shard_map/ppermute | solution.py:39
  352.9 11.5 %collective-permute-start.81 = (f32[384,256]{1,0:T(8,128)S(1)}, f32[384,256]{1,0:T(8,128)S(1)}, u32[]{:S(2)}, u32[]{:S(2)}) collective-permute-start(f32[384,256]{1,0:T(8,128)S(1)} %get-tuple-element.125), channel_id=1, source_target_pairs={{0,2},{2,0},{1,3},{3,1},{4,6},{6,4},{5,7},{7,5},{8,10},{10,8},{9,1... | collective-permute-start | bytes 1179656 | tf_op jit(solution)/shard_map/ppermute | solution.py:39
  355.2 32.7 %collective-permute-start.58 = (f32[192,256]{1,0:T(8,128)S(1)}, f32[192,256]{1,0:T(8,128)S(1)}, u32[]{:S(2)}, u32[]{:S(2)}) collective-permute-start(f32[192,256]{1,0:T(8,128)S(1)} %slice_select_fusion.5), channel_id=1, source_target_pairs={{0,1},{1,0},{2,3},{3,2},{4,5},{5,4},{6,7},{7,6},{8,9},{9,8},{10,11... | collective-permute-start | bytes 589832 | tf_op jit(solution)/shard_map/ppermute | solution.py:39
  355.3 49.3 %collective-permute-start.89 = (f32[3072,256]{1,0:T(8,128)}, f32[3072,256]{1,0:T(8,128)}, u32[]{:S(2)}, u32[]{:S(2)}) collective-permute-start(f32[3072,256]{1,0:T(8,128)} %bitcast.74), channel_id=1, source_target_pairs={{0,1},{1,0},{2,3},{3,2},{4,5},{5,4},{6,7},{7,6},{8,9},{9,8},{10,11... | collective-permute-start | bytes 9437192 | tf_op jit(solution)/shard_map/ppermute | solution.py:39
  355.8 13.2 %collective-permute-start.83 = (f32[384,256]{1,0:T(8,128)S(1)}, f32[384,256]{1,0:T(8,128)S(1)}, u32[]{:S(2)}, u32[]{:S(2)}) collective-permute-start(f32[384,256]{1,0:T(8,128)S(1)} %get-tuple-element.125), channel_id=1, source_target_pairs={{0,12},{4,0},{8,4},{12,8},{1,13},{5,1},{9,5},{13,9},{2,14},{6,2},{... | collective-permute-start | bytes 1179656 | tf_op jit(solution)/shard_map/ppermute | solution.py:39
  364.5 12.9 %collective-permute-start.84 = (f32[384,256]{1,0:T(8,128)S(1)}, f32[384,256]{1,0:T(8,128)S(1)}, u32[]{:S(2)}, u32[]{:S(2)}) collective-permute-start(f32[384,256]{1,0:T(8,128)S(1)} %collective-permute-done.82), channel_id=1, source_target_pairs={{0,4},{4,8},{8,12},{12,0},{1,5},{5,9},{9,13},{13,1},{2,6},{6,10},{... | collective-permute-start | bytes 1179656 | tf_op jit(solution)/shard_map/ppermute | solution.py:39
  364.5 12.1 %collective-permute-start.86 = (f32[384,256]{1,0:T(8,128)S(1)}, f32[384,256]{1,0:T(8,128)S(1)}, u32[]{:S(2)}, u32[]{:S(2)}) collective-permute-start(f32[384,256]{1,0:T(8,128)S(1)} %collective-permute-done.81), channel_id=1, source_target_pairs={{0,12},{4,0},{8,4},{12,8},{1,13},{5,1},{9,5},{13,9},{2,14},{6,2},{... | collective-permute-start | bytes 1179656 | tf_op jit(solution)/shard_map/ppermute | solution.py:39
  369.0 11.7 %collective-permute-start.85 = (f32[384,256]{1,0:T(8,128)S(1)}, f32[384,256]{1,0:T(8,128)S(1)}, u32[]{:S(2)}, u32[]{:S(2)}) collective-permute-start(f32[384,256]{1,0:T(8,128)S(1)} %collective-permute-done.81), channel_id=1, source_target_pairs={{0,4},{4,8},{8,12},{12,0},{1,5},{5,9},{9,13},{13,1},{2,6},{6,10},{... | collective-permute-start | bytes 1179656 | tf_op jit(solution)/shard_map/ppermute | solution.py:39
  387.8 42.4 %collective-permute-start.103 = (f32[3072,256]{1,0:T(8,128)S(1)}, f32[3072,256]{1,0:T(8,128)}, u32[]{:S(2)}, u32[]{:S(2)}) collective-permute-start(f32[3072,256]{1,0:T(8,128)S(1)} %bitcast.178), channel_id=1, source_target_pairs={{0,1},{1,0},{2,3},{3,2},{4,5},{5,4},{6,7},{7,6},{8,9},{9,8},{10,11... | collective-permute-start | bytes 9437192 | tf_op jit(solution)/shard_map/ppermute | solution.py:39
  397.5 32.7 %collective-permute-start.102 = (f32[192,256]{1,0:T(8,128)S(1)}, f32[192,256]{1,0:T(8,128)S(1)}, u32[]{:S(2)}, u32[]{:S(2)}) collective-permute-start(f32[192,256]{1,0:T(8,128)S(1)} %get-tuple-element.50), channel_id=1, source_target_pairs={{0,1},{1,0},{2,3},{3,2},{4,5},{5,4},{6,7},{7,6},{8,9},{9,8},{10,11... | collective-permute-start | bytes 589832 | tf_op jit(solution)/shard_map/ppermute | solution.py:39
  421.0 25.7 %collective-permute-start.93 = (f32[192,384]{1,0:T(8,128)S(1)}, f32[192,384]{1,0:T(8,128)S(1)}, u32[]{:S(2)}, u32[]{:S(2)}) collective-permute-start(f32[192,384]{1,0:T(8,128)S(1)} %fusion.84), channel_id=1, source_target_pairs={{0,16},{16,32},{32,48},{48,0},{1,17},{17,33},{33,49},{49,1},{2,18}... | collective-permute-start | bytes 884744 | tf_op jit(solution)/shard_map/ppermute | solution.py:39
  424.6 25.0 %collective-permute-start.95 = (f32[192,384]{1,0:T(8,128)S(1)}, f32[192,384]{1,0:T(8,128)S(1)}, u32[]{:S(2)}, u32[]{:S(2)}) collective-permute-start(f32[192,384]{1,0:T(8,128)S(1)} %convolution_add_fusion.4), channel_id=1, source_target_pairs={{0,48},{16,0},{32,16},{48,32},{1,49},{17,1},{33,17},{49,33},{2,50}... | collective-permute-start | bytes 884744 | tf_op jit(solution)/shard_map/ppermute | solution.py:39
  433.3 20.6 %collective-permute-start.107 = (f32[192,384]{1,0:T(8,128)S(1)}, f32[192,384]{1,0:T(8,128)S(1)}, u32[]{:S(2)}, u32[]{:S(2)}) collective-permute-start(f32[192,384]{1,0:T(8,128)S(1)} %fusion.64), channel_id=1, source_target_pairs={{0,16},{16,32},{32,48},{48,0},{1,17},{17,33},{33,49},{49,1},{2,18}... | collective-permute-start | bytes 884744 | tf_op jit(solution)/shard_map/ppermute | solution.py:39
  (81 other events, 622.1 us)
